TPU v7x, 256 devices: a whole 4x4x8 slice. The times are simulated.
256 devices in a mesh: section: 2 (over core), rep: 8 (over z_lo, x), tp: 16 (over z_hi, y).
Axes of the slice: x: 4, y: 4, z: 8 (z_hi: 4, z_lo: 2; z = z_hi * 2 + z_lo), core: 2. Of those that a mesh axis runs over, the one named last changes fastest.
Arguments:
- states: bfloat16 [2, 8, 256, 8192], P('section', 'rep', None, 'tp'), may hold values from -6 to 6
- q_weight: bfloat16 [8192, 4096], P(None, 'tp'), may hold values from -0.0625 to 0.0625
- kv_weight: bfloat16 [8192, 1024], P('tp'), may hold values from -0.0625 to 0.0625
- o_weight: bfloat16 [4096, 8192], P(None, 'tp'), may hold values from -0.09375 to 0.09375
- store_keys: bfloat16 [2, 8, 4096, 512], P('section', 'rep', 'tp'), may hold values from -170 to 170
- store_values: bfloat16 [2, 8, 4096, 512], P('section', 'rep', 'tp'), may hold values from -48 to 48
- prefix_len: int32 [8], replicated, may hold values from 1024 to 4096
- cache_len: int32 [8, 4], P('rep'), may hold values from 128 to 1024
- parents: int32 [8, 4, 64], P('rep'), may hold values from -1 to 62, as said below
Outputs:
- attn_out: bfloat16 [2, 8, 256, 8192], P('section', 'rep', None, 'tp')
Inputs may be any that keep to these rules, and one draw needn't show every extreme that they name: `parents`: each node's parent is an earlier node of the same tree; only node 0 has -1.
All inputs are finite; a program needn't handle non-finite values.
Results may differ from a plain program's by a relative error of at most 0.0065.
The roundings to bfloat16 on the way count: a program that leaves them out, or rounds other values in their place, can miss the bound.
Values may be sent and summed in bfloat16 or wider, within the bound.
A program may use at most 64 MiB of HBM per device.

v0:
```python
import jax
import jax.numpy as jnp
from jax import lax
from jax.sharding import Mesh
from jax.sharding import PartitionSpec as P

HD = 128
SEQS = 4
NODES = 64
CACHE = 1024
TP = ("tp_0", "tp_1")
ROPE_BASE = 500000.0
MASKED_SCORE = -1e30


def in_blocks(shard, dim, devices):
    before, after = (shard.shape[:dim], shard.shape[dim + 1 :])
    return jnp.moveaxis(shard.reshape(*before, devices, -1, *after), dim, 0)


def summed_on_arrival(shard, axis, dim):
    tiles = in_blocks(shard, dim, lax.axis_size(axis))
    arrived = lax.all_to_all(tiles, axis, split_axis=0, concat_axis=0, tiled=True)
    return arrived.astype(jnp.float32).sum(axis=0)


def passed_along(block, axis, distance):
    devices = range(lax.axis_size(axis))
    route = [(i - distance, i) for i in devices if i - distance in devices]
    return lax.ppermute(block, axis, route)


def joined_along(tiles, dim):
    lengths = list(tiles.shape[1:])
    lengths[dim] *= tiles.shape[0]
    return jnp.moveaxis(tiles, 0, dim).reshape(lengths)


def exchange_in_order(tiles, axes, order):
    lengths = [lax.axis_size(a) for a in axes]
    tiles = tiles.reshape(*lengths, *tiles.shape[1:])
    for k in order:
        tiles = lax.all_to_all(tiles, axes[k], split_axis=k, concat_axis=k, tiled=True)
    return tiles.reshape(-1, *tiles.shape[len(axes) :])


def exchange_by_axis(shard, axes, order, split_dim, concat_dim):
    tiles = in_blocks(shard, split_dim, lax.axis_size(axes))
    return joined_along(exchange_in_order(tiles, axes, order), concat_dim)


def rotate(vectors, positions):
    head_size = vectors.shape[-1]
    half_width = head_size // 2
    exponent = jnp.arange(half_width, dtype=jnp.float32) * (-2.0 / head_size)
    frequency = jnp.exp(exponent * jnp.log(jnp.float32(ROPE_BASE)))
    angles = positions.astype(jnp.float32)[:, None] * frequency[None, :]
    cosine = jnp.cos(angles)[:, None, :]
    sine_of = jnp.sin(angles)[:, None, :]
    front_half = vectors[..., :half_width]
    back_half = vectors[..., half_width:]
    return jnp.concatenate(
        [front_half * cosine - back_half * sine_of, back_half * cosine + front_half * sine_of],
        axis=-1,
    )


def closure(parents):
    node_count = parents.shape[-1]
    node_ids = jnp.arange(node_count, dtype=jnp.int32)
    reached = (parents[:, :, None] == node_ids[None, None, :]).astype(jnp.float32)
    reached = reached + jnp.eye(node_count, dtype=jnp.float32)[None]
    for level_index in range(max(1, (node_count - 1).bit_length())):
        reached = jnp.minimum(
            jnp.einsum("sij,sjk->sik", reached, reached, precision=lax.Precision.HIGHEST), 1.0
        )
    return reached


def partial_attend(queries, all_keys, all_values, visible):
    row_count = queries.shape[0]
    kv_heads = all_keys.shape[1] // HD
    group_size = queries.shape[1] // all_keys.shape[1]
    row_tops = []
    row_totals = []
    mixtures = []
    for kv_head in range(kv_heads):
        query_block = queries[
            :, kv_head * group_size * HD : (kv_head + 1) * group_size * HD
        ].reshape(row_count * group_size, HD)
        key_block = all_keys[:, kv_head * HD : (kv_head + 1) * HD]
        value_block = all_values[:, kv_head * HD : (kv_head + 1) * HD]
        scores = lax.dot_general(
            query_block, key_block, (((1,), (1,)), ((), ())), preferred_element_type=jnp.float32
        )
        scores = scores.reshape(row_count, group_size, -1) * HD ** (-0.5)
        scores = jnp.where(visible[:, None, :], scores, MASKED_SCORE)
        row_top = jnp.max(scores, axis=-1)
        weights = jnp.where(visible[:, None, :], jnp.exp(scores - row_top[..., None]), 0.0)
        row_total = jnp.sum(weights, axis=-1)
        mixed_rows = jnp.dot(
            weights.astype(jnp.bfloat16).reshape(row_count * group_size, -1),
            value_block,
            preferred_element_type=jnp.float32,
        )
        mixed_rows = (
            mixed_rows.reshape(row_count, group_size, HD) / jnp.maximum(row_total, 1.0)[..., None]
        )
        row_tops.append(row_top)
        row_totals.append(row_total)
        mixtures.append(mixed_rows.reshape(row_count, group_size * HD).astype(jnp.bfloat16))
    return (
        jnp.concatenate(row_tops, axis=1),
        jnp.concatenate(row_totals, axis=1),
        jnp.concatenate(mixtures, axis=1),
    )


def finish(tops, totals, parts):
    piece_count, row_count, head_count = tops.shape
    best = jnp.max(tops, axis=0)
    factor = jnp.exp(tops - best[None]) * totals
    denominator = jnp.sum(factor, axis=0)
    numerator = jnp.sum(
        parts.astype(jnp.float32).reshape(piece_count, row_count, head_count, HD)
        * factor[..., None],
        axis=0,
    )
    return (
        (numerator / denominator[..., None])
        .reshape(row_count, head_count * HD)
        .astype(jnp.bfloat16)
    )


def per_device(
    states, q_weight, kv_weight, o_weight, store_keys, store_values, prefix_len, cache_len, parents
):
    inputs = states[0, 0]
    row_count = inputs.shape[0]
    tp_count = lax.axis_size(TP)
    tp_index = lax.axis_index(TP)
    replica = lax.axis_index("rep")
    rep_count = lax.axis_size("rep")
    decoding = lax.axis_index("section") == 1
    own_cols = q_weight.shape[1]
    kv_width = kv_weight.shape[1] // 2
    block_rows = row_count // tp_count
    first_row = tp_index * block_rows
    row_ids = jnp.arange(row_count, dtype=jnp.int32)
    seq_of = row_ids // NODES
    own_prefix = prefix_len[replica]
    reached = closure(parents[0])
    depths = (jnp.sum(reached, axis=-1).astype(jnp.int32) - 1).reshape(row_count)
    seq_lengths = jnp.broadcast_to(cache_len[0][:, None], (SEQS, NODES)).reshape(row_count)
    tree_base = jnp.where(seq_of == 0, own_prefix + row_count, seq_lengths)
    positions = jnp.where(decoding, tree_base + depths, own_prefix + row_ids)
    weight_rows = q_weight
    query_sums = jnp.dot(
        lax.all_gather(inputs, TP, axis=1, tiled=True),
        weight_rows,
        preferred_element_type=jnp.float32,
    )
    own_queries = (
        rotate(query_sums.reshape(row_count, own_cols // HD, HD), positions)
        .reshape(row_count, own_cols)
        .astype(jnp.bfloat16)
    )
    queries = lax.all_gather(own_queries, TP, axis=1, tiled=True)
    kv_rows = summed_on_arrival(
        jnp.dot(inputs, kv_weight, preferred_element_type=jnp.float32).astype(jnp.bfloat16), TP, 0
    )
    local_pos = lax.dynamic_slice_in_dim(positions, first_row, block_rows, 0)
    new_keys = (
        rotate(kv_rows[:, :kv_width].reshape(block_rows, -1, HD), local_pos)
        .reshape(block_rows, kv_width)
        .astype(jnp.bfloat16)
    )
    new_values = kv_rows[:, kv_width:].astype(jnp.bfloat16)
    moved = passed_along(jnp.stack([new_keys, new_values]), ("section", "rep"), rep_count)
    tail_keys = moved[0]
    tail_values = moved[1]
    store_rows = store_keys.shape[2]
    store_pos = tp_index * store_rows + jnp.arange(store_rows, dtype=jnp.int32)
    prefill_store = jnp.broadcast_to(store_pos[None, :] < own_prefix, (row_count, store_rows))
    decode_store = (store_pos[None, :] // CACHE == seq_of[:, None]) & (
        store_pos[None, :] % CACHE < seq_lengths[:, None]
    )
    block_ids = first_row + jnp.arange(block_rows, dtype=jnp.int32)
    prefill_new = block_ids[None, :] <= row_ids[:, None]
    eye_seq = (jnp.arange(SEQS)[:, None] == jnp.arange(SEQS)[None, :]).astype(jnp.float32)
    tree_full = (eye_seq[:, None, :, None] * reached[:, :, None, :]).reshape(row_count, row_count)
    decode_new = lax.dynamic_slice_in_dim(tree_full, first_row, block_rows, 1) > 0.5
    tail_seen = jnp.broadcast_to((seq_of == 0)[:, None], (row_count, block_rows))
    decode_mask = jnp.concatenate([decode_store, decode_new, tail_seen], axis=1)
    prefill_mask = jnp.concatenate([prefill_store, prefill_new, jnp.zeros_like(tail_seen)], axis=1)
    visible = jnp.where(decoding, decode_mask, prefill_mask)
    all_keys = jnp.concatenate([store_keys[0, 0], new_keys, tail_keys], axis=0)
    all_values = jnp.concatenate([store_values[0, 0], new_values, tail_values], axis=0)
    row_tops, row_totals, mixtures = partial_attend(queries, all_keys, all_values, visible)
    peer_tops, peer_totals, peer_mix = (
        exchange_by_axis(row_tops[None], TP, (0, 1), 2, 0),
        exchange_by_axis(row_totals[None], TP, (0, 1), 2, 0),
        exchange_by_axis(mixtures[None].astype(jnp.float32), TP, (0, 1), 2, 0).astype(jnp.bfloat16),
    )
    own_attended = finish(peer_tops, peer_totals, peer_mix)
    weight_rows = o_weight
    result = jnp.dot(
        lax.all_gather(own_attended, TP, axis=1, tiled=True),
        weight_rows,
        preferred_element_type=jnp.float32,
    )
    return result.astype(jnp.bfloat16)[None, None]


def solution(mesh):
    split = Mesh(
        mesh.devices.reshape(mesh.shape["section"], mesh.shape["rep"], 4, 4),
        ("section", "rep", "tp_0", "tp_1"),
    )
    placed = (
        P("section", "rep", None, TP),
        P(None, TP),
        P(TP, None),
        P(None, TP),
        P("section", "rep", TP, None),
        P("section", "rep", TP, None),
        P(),
        P("rep", None),
        P("rep", None, None),
    )
    return jax.shard_map(
        per_device,
        mesh=split,
        in_specs=placed,
        out_specs=P("section", "rep", None, TP),
        check_vma=False,
    )
```

profile of v0, /device:TPU:2, one launch (start us, length us, event | category | flops | bytes accessed | tf_op | source)
XLA Modules:
  0.0 364.5 jit_solution(4483975345601718534)
XLA Ops:
  6.5 0.7 all-gather.9.cloned.1.call-update
  7.3 0.7 broadcast_in_dim.55
  8.1 1.1 convolution_minimum_fusion.5
  10.8 0.7 dynamic_slice.10
  12.1 0.7 fusion.70
  13.1 81.5 %all-gather.9.cloned.1.call-done = bf16[1,1,256,8192]{3,2,1,0:T(8,128)(2,1)} async-done(((bf16[1,1,256,512]{3,2,1,0:T(8,128)(2,1)}), bf16[1,1,256,8192]{3,2,1,0:T(8,128)(2,1)}) %all-gather.9.cloned.1.call-update) | async-done | bytes 4194320 | tf_op jit(solution)/shard_map/all_gather | solution.py:160
  94.6 5.2 %fusion = f32[256,256]{0,1:T(8,128)S(1)} fusion(bf16[8192,256]{1,0:T(8,128)(2,1)} %param.10, bf16[1,1,256,8192]{3,2,1,0:T(8,128)(2,1)} %all-gather.9.cloned.1.call-done), kind=kOutput, calls=%fused_computation | convolution fusion | flops 1073741824 | bytes 8650752 | tf_op jit(solution)/shard_map/dot_general | solution.py:159
  99.9 0.7 pad_maximum_fusion.2
  100.6 1.2 convolution_convert_fusion
  101.8 6.2 %all-to-all-start = ((bf16[16,16,1024]{2,1,0:T(8,128)(2,1)}), bf16[16,16,1024]{2,1,0:T(8,128)(2,1)S(1)}, u32[]{:S(2)}, u32[]{:S(2)}) async-start(bf16[16,16,1024]{2,1,0:T(8,128)(2,1)} %bitcast.9), calls=%async_computation | async-start | bytes 1048576 | tf_op jit(solution)/shard_map/all_to_all | solution.py:23
  108.1 0.7 fusion.56
  110.0 18.6 %all-to-all-done = bf16[16,16,1024]{2,1,0:T(8,128)(2,1)S(1)} async-done(((bf16[16,16,1024]{2,1,0:T(8,128)(2,1)}), bf16[16,16,1024]{2,1,0:T(8,128)(2,1)S(1)}, u32[]{:S(2)}, u32[]{:S(2)}) %all-to-all-start) | async-done | bytes 524320 | tf_op jit(solution)/shard_map/all_to_all | solution.py:23
  128.9 1.3 collective-permute-start
  130.4 0.6 collective-permute-done
  131.1 0.9 pad_maximum_fusion
  131.9 31.4 %all-gather.5.cloned.1.call-done = bf16[256,4096]{0,1:T(8,128)(2,1)} async-done(((bf16[256,256]{0,1:T(8,128)(2,1)}), bf16[256,4096]{0,1:T(8,128)(2,1)}) %all-gather.5.cloned.1.call-update) | async-done | bytes 2097168 | tf_op jit(solution)/shard_map/all_gather | solution.py:169
  163.3 1.7 fusion.71
  165.0 0.5 fusion.47
  166.0 0.5 fusion.2
  166.5 3.3 fusion.6
  169.8 0.6 broadcast_maximum_fusion.3
  170.4 0.6 reshape_broadcast_in_dim.6
  171.0 4.7 %all-to-all-start.3 = ((f32[4,4,1,256,2]{3,4,1,2,0:T(2,128)}), f32[4,4,1,256,2]{3,4,1,2,0:T(2,128)S(1)}, u32[]{:S(2)}, u32[]{:S(2)}) async-start(f32[4,4,1,256,2]{3,4,1,2,0:T(2,128)} %bitcast.32), calls=%async_computation.3 | async-start | bytes 65536 | tf_op jit(solution)/shard_map/all_to_all | solution.py:43
  175.7 4.3 %fusion.8 = (f32[256,8]{0,1:T(8,128)S(1)}, f32[256,8]{0,1:T(8,128)S(1)}, f32[256,8]{0,1:T(8,128)S(1)}) fusion(f32[256,8,288]{0,2,1:T(8,128)} %get-tuple-element.32, f32[256,8]{0,1:T(8,128)S(1)} %get-tuple-element.6, pred[256,288]{0,1:T(8,128)(4,1)S(1)} %add_select_fusion, f32[256,8]{0,1:T(8,128)S(1)} %get-tuple-element.7, f32[256,8,288]{0,2,1:T(8,128)} %copy-done.1, ...), kind=kLoop, calls=%fused_computation.19 | loop fusion | flops 8841216 | bytes 7200768 | tf_op jit(solution)/shard_map/reduce_sum | solution.py:100
  180.0 1.6 fusion.14
  181.7 1.6 fusion.15
  183.3 1.6 fusion.16
  184.9 0.6 broadcast_maximum_fusion
  185.5 0.6 reshape_broadcast_in_dim.7
  186.2 7.2 %all-to-all-start.5 = ((f32[4,4,1,256,2]{3,4,1,2,0:T(2,128)}), f32[4,4,1,256,2]{3,4,1,2,0:T(2,128)S(1)}, u32[]{:S(2)}, u32[]{:S(2)}) async-start(f32[4,4,1,256,2]{3,4,1,2,0:T(2,128)} %bitcast.123), calls=%async_computation.5 | async-start | bytes 65536 | tf_op jit(solution)/shard_map/all_to_all | solution.py:43
  193.3 2.5 fusion.17
  195.8 0.6 copy.40
  196.4 4.8 %all-to-all-done.5 = f32[4,4,1,256,2]{3,4,1,2,0:T(2,128)S(1)} async-done(((f32[4,4,1,256,2]{3,4,1,2,0:T(2,128)}), f32[4,4,1,256,2]{3,4,1,2,0:T(2,128)S(1)}, u32[]{:S(2)}, u32[]{:S(2)}) %all-to-all-start.5) | async-done | bytes 32800 | tf_op jit(solution)/shard_map/all_to_all | solution.py:43
  201.2 3.4 all-to-all-start.4
  204.6 3.1 maximum_convert_fusion
  207.7 2.3 all-to-all-done.4
  210.0 3.6 all-to-all-start.1
  213.7 0.6 copy.42
  214.3 45.5 %all-to-all-done.1 = bf16[4,4,1,256,256]{3,4,1,2,0:T(8,128)(2,1)S(1)} async-done(((bf16[4,4,1,256,256]{3,4,1,2,0:T(8,128)(2,1)}), bf16[4,4,1,256,256]{3,4,1,2,0:T(8,128)(2,1)S(1)}, u32[]{:S(2)}, u32[]{:S(2)}) %all-to-all-start.1) | async-done | bytes 2097184 | tf_op jit(solution)/shard_map/all_to_all | solution.py:43
  259.8 3.4 all-to-all-start.6
  263.1 1.5 copy.38
  264.6 4.0 %all-to-all-done.6 = f32[4,4,1,256,2]{3,4,0,2,1:T(2,128)S(1)} async-done(((f32[4,4,1,256,2]{3,4,0,2,1:T(2,128)}), f32[4,4,1,256,2]{3,4,0,2,1:T(2,128)S(1)}, u32[]{:S(2)}, u32[]{:S(2)}) %all-to-all-start.6) | async-done | bytes 32800 | tf_op jit(solution)/shard_map/all_to_all | solution.py:43
  268.6 3.6 all-to-all-start.2
  272.4 22.8 %all-to-all-done.2 = bf16[4,4,1,256,256]{3,4,0,2,1:T(8,128)(2,1)S(1)} async-done(((bf16[4,4,1,256,256]{3,4,0,2,1:T(8,128)(2,1)}), bf16[4,4,1,256,256]{3,4,0,2,1:T(8,128)(2,1)S(1)}, u32[]{:S(2)}, u32[]{:S(2)}) %all-to-all-start.2) | async-done | bytes 2097184 | tf_op jit(solution)/shard_map/all_to_all | solution.py:43
  295.5 0.5 multiply_reduce_fusion
  296.0 0.7 fusion.43
  296.7 56.5 %all-gather.7.cloned.1.call-done = bf16[256,4096]{0,1:T(8,128)(2,1)} async-done(((bf16[256,256]{0,1:T(8,128)(2,1)}), bf16[256,4096]{0,1:T(8,128)(2,1)}) %all-gather.7.cloned.1.call-update) | async-done | bytes 2097168 | tf_op jit(solution)/shard_map/all_gather | solution.py:209
  353.2 4.8 %fusion.42 = bf16[1,1,256,512]{3,2,1,0:T(8,128)(2,1)} fusion(bf16[256,4096]{0,1:T(8,128)(2,1)} %all-gather.7.cloned.1.call-done, bf16[4096,512]{1,0:T(8,128)(2,1)} %param.12), kind=kOutput, calls=%fused_computation.55 | convolution fusion | flops 1073872896 | bytes 6553600 | tf_op jit(solution)/shard_map/dot_general | solution.py:208
  (85 shorter events, 4.7 us)
Async XLA Ops:
  6.5 94.0 %copy-start = (bf16[512,1024]{1,0:T(8,128)(2,1)S(1)}, bf16[512,1024]{1,0:T(8,128)(2,1)}, u32[]{:S(2)}) copy-start(bf16[512,1024]{1,0:T(8,128)(2,1)} %param.11) | copy-start | bytes 3145732
  6.5 4.2 %copy-start.13 = (s32[8]{0:T(128)S(1)}, s32[8]{0:T(128)}, u32[]{:S(2)}) copy-start(s32[8]{0:T(128)} %param.15) | copy-start | bytes 100
  6.5 88.1 %all-gather.9.cloned.1.call-start = ((), (), s32[]{:S(2)}) async-start(), calls=%async_computation.9 | async-start | bytes 4456448 | tf_op jit(solution)/shard_map/all_gather | solution.py:160
  7.3 156.1 %all-gather.5.cloned.1.call-start = ((), (), s32[]{:S(2)}) async-start(), calls=%async_computation.7 | async-start | bytes 2228224 | tf_op jit(solution)/shard_map/all_gather | solution.py:169
  13.1 87.5 %copy-start.6 = (bf16[1,1,256,512]{3,2,1,0:T(8,128)(2,1)S(1)}, bf16[1,1,256,512]{3,2,1,0:T(8,128)(2,1)}, u32[]{:S(2)}) copy-start(bf16[1,1,256,512]{3,2,1,0:T(8,128)(2,1)} %param.9) | copy-start | bytes 786436
  101.8 29.2 %copy-start.9 = (bf16[1,1,256,512]{3,2,1,0:T(8,128)(2,1)S(1)}, bf16[1,1,256,512]{3,2,1,0:T(8,128)(2,1)}, u32[]{:S(2)}) copy-start(bf16[1,1,256,512]{3,2,1,0:T(8,128)(2,1)} %param.13) | copy-start | bytes 786436
  101.8 29.2 %copy-start.10 = (bf16[1,1,256,512]{3,2,1,0:T(8,128)(2,1)S(1)}, bf16[1,1,256,512]{3,2,1,0:T(8,128)(2,1)}, u32[]{:S(2)}) copy-start(bf16[1,1,256,512]{3,2,1,0:T(8,128)(2,1)} %param.14) | copy-start | bytes 786436
  101.8 26.7 %all-to-all-start = ((bf16[16,16,1024]{2,1,0:T(8,128)(2,1)}), bf16[16,16,1024]{2,1,0:T(8,128)(2,1)S(1)}, u32[]{:S(2)}, u32[]{:S(2)}) async-start(bf16[16,16,1024]{2,1,0:T(8,128)(2,1)} %bitcast.9), calls=%async_computation | async-start | bytes 1048576 | tf_op jit(solution)/shard_map/all_to_all | solution.py:23
  128.9 2.1 collective-permute-start
  163.3 1.7 copy-start.7
  166.0 3.8 %copy-start.1 = (f32[256,8,288]{0,2,1:T(8,128)}, f32[256,8,288]{0,2,1:T(8,128)S(1)}, u32[]{:S(2)}) copy-start(f32[256,8,288]{0,2,1:T(8,128)S(1)} %fusion.48) | copy-start | bytes 7077892
  166.5 3.3 copy-start.3
  169.8 10.2 %copy-start.11 = (f32[256,8]{0,1:T(8,128)}, f32[256,8]{0,1:T(8,128)S(1)}, u32[]{:S(2)}) copy-start(f32[256,8]{0,1:T(8,128)S(1)} %get-tuple-element.8) | copy-start | bytes 24580
  171.0 15.2 %all-to-all-start.3 = ((f32[4,4,1,256,2]{3,4,1,2,0:T(2,128)}), f32[4,4,1,256,2]{3,4,1,2,0:T(2,128)S(1)}, u32[]{:S(2)}, u32[]{:S(2)}) async-start(f32[4,4,1,256,2]{3,4,1,2,0:T(2,128)} %bitcast.32), calls=%async_computation.3 | async-start | bytes 65536 | tf_op jit(solution)/shard_map/all_to_all | solution.py:43
  175.6 4.3 %copy-start.4 = (f32[256,8,288]{0,2,1:T(8,128)S(1)}, f32[256,8,288]{0,2,1:T(8,128)}, u32[]{:S(2)}) copy-start(f32[256,8,288]{0,2,1:T(8,128)} %copy-done.3) | copy-start | bytes 7077892
  175.7 4.3 %copy-start.8 = (bf16[288,512]{1,0:T(8,128)(2,1)S(1)}, bf16[288,512]{1,0:T(8,128)(2,1)}, u32[]{:S(2)}) copy-start(bf16[288,512]{1,0:T(8,128)(2,1)} %get-tuple-element.38) | copy-start | bytes 884740
  175.7 4.3 %copy-start.12 = (f32[256,8]{0,1:T(8,128)S(1)}, f32[256,8]{0,1:T(8,128)}, u32[]{:S(2)}) copy-start(f32[256,8]{0,1:T(8,128)} %broadcast_maximum_fusion.3) | copy-start | bytes 24580
  180.0 1.7 copy-start.5
  181.7 1.7 copy-start.2
  186.2 15.1 %all-to-all-start.5 = ((f32[4,4,1,256,2]{3,4,1,2,0:T(2,128)}), f32[4,4,1,256,2]{3,4,1,2,0:T(2,128)S(1)}, u32[]{:S(2)}, u32[]{:S(2)}) async-start(f32[4,4,1,256,2]{3,4,1,2,0:T(2,128)} %bitcast.123), calls=%async_computation.5 | async-start | bytes 65536 | tf_op jit(solution)/shard_map/all_to_all | solution.py:43
  201.2 8.8 %all-to-all-start.4 = ((f32[4,4,1,256,2]{3,4,0,2,1:T(2,128)}), f32[4,4,1,256,2]{3,4,0,2,1:T(2,128)S(1)}, u32[]{:S(2)}, u32[]{:S(2)}) async-start(f32[4,4,1,256,2]{3,4,0,2,1:T(2,128)} %copy.40), calls=%async_computation.4 | async-start | bytes 65536 | tf_op jit(solution)/shard_map/all_to_all | solution.py:43
  210.0 49.7 %all-to-all-start.1 = ((bf16[4,4,1,256,256]{3,4,1,2,0:T(8,128)(2,1)}), bf16[4,4,1,256,256]{3,4,1,2,0:T(8,128)(2,1)S(1)}, u32[]{:S(2)}, u32[]{:S(2)}) async-start(bf16[4,4,1,256,256]{3,4,1,2,0:T(8,128)(2,1)} %bitcast.109), calls=%async_computation.1 | async-start | bytes 4194304 | tf_op jit(solution)/shard_map/all_to_all | solution.py:43
  259.8 8.8 %all-to-all-start.6 = ((f32[4,4,1,256,2]{3,4,0,2,1:T(2,128)}), f32[4,4,1,256,2]{3,4,0,2,1:T(2,128)S(1)}, u32[]{:S(2)}, u32[]{:S(2)}) async-start(f32[4,4,1,256,2]{3,4,0,2,1:T(2,128)} %copy.42), calls=%async_computation.6 | async-start | bytes 65536 | tf_op jit(solution)/shard_map/all_to_all | solution.py:43
  268.6 26.6 %all-to-all-start.2 = ((bf16[4,4,1,256,256]{3,4,0,2,1:T(8,128)(2,1)}), bf16[4,4,1,256,256]{3,4,0,2,1:T(8,128)(2,1)S(1)}, u32[]{:S(2)}, u32[]{:S(2)}) async-start(bf16[4,4,1,256,256]{3,4,0,2,1:T(8,128)(2,1)} %copy.38), calls=%async_computation.2 | async-start | bytes 4194304 | tf_op jit(solution)/shard_map/all_to_all | solution.py:43
  272.2 81.0 %all-gather.7.cloned.1.call-start = ((), (), s32[]{:S(2)}) async-start(), calls=%async_computation.8 | async-start | bytes 2228224 | tf_op jit(solution)/shard_map/all_gather | solution.py:209
Sparse Core Ops, SparseCore 0:
  9.7 84.8 all-gather.8
  100.7 62.5 all-gather.4
  296.9 56.3 all-gather.6
where the time goes:
time: 365 us
  waiting for transfers between devices  269 us (74%)
  starting transfers between devices  33.4 us (9%)
  matrix products  25.7 us (7%)
  between operations  14.2 us (4%)
  other arithmetic  14.1 us (4%)
  local copies, waits for them, and re-layouts  8.3 us (2%)
    all_gather x1, waiting for transfers between devices, per_device(): lax.all_gather(inputs, TP, axis=1, tiled=True)  81.5 us
    all_to_all x6, waiting for transfers between devices, exchange_in_order(): lax.all_to_all(tiles, axes[k], split_axis=k, concat_axis=k, tiled=True)  79.4 us
    all_gather x1, waiting for transfers between devices, per_device(): lax.all_gather(own_attended, TP, axis=1, tiled=True)  56.5 us
    all_gather x1, waiting for transfers between devices, per_device(): queries = lax.all_gather(own_queries, TP, axis=1, tiled=True)  31.4 us
    all_to_all x6, starting transfers between devices, exchange_in_order(): lax.all_to_all(tiles, axes[k], split_axis=k, concat_axis=k, tiled=True)  25.8 us
    all_to_all x1, waiting for transfers between devices, summed_on_arrival(): lax.all_to_all(tiles, axis, split_axis=0, concat_axis=0, tiled=True)  18.6 us
  transfers between devices with their start and end apart: 11, of which 10 were waited for; matrix products, arithmetic and copies ran while one was open for 8% of the time, Pallas kernels for 0%

commit v1 on v0

--- a/solution.py
+++ b/solution.py
@@ -157,7 +157,7 @@
     positions = jnp.where(decoding, tree_base + depths, own_prefix + row_ids)
     weight_rows = q_weight
     query_sums = jnp.dot(
-        lax.all_gather(inputs, TP, axis=1, tiled=True),
+        jnp.concatenate(lax.all_to_all(jnp.stack([inputs] * lax.axis_size(TP)), TP, 0, 0), axis=1),
         weight_rows,
         preferred_element_type=jnp.float32,
     )

time: 365 us -> 402 us (1.10)
  local copies, waits for them, and re-layouts: 8.3 us -> 32.1 us
  starting transfers between devices: 33.4 us -> 48.4 us
    all_to_all x0 -> x1, waiting for transfers between devices: none -> 83.2 us  [per_device(): lax.all_to_all(jnp.stack([inputs] * lax.axis_size(TP)), TP, 0, 0)]
    all_gather x1 -> x0, waiting for transfers between devices: 81.5 us -> none  [per_device(): lax.all_gather(inputs, TP, axis=1, tiled=True)]
    reshape x0 -> x2, local copies, waits for them, and re-layouts: none -> 13.9 us  [per_device(): jnp.concatenate(lax.all_to_all(jnp.stack([inputs] * lax.axis_size(TP)), T...]
    all_to_all x0 -> x1, starting transfers between devices: none -> 11.4 us  [per_device(): lax.all_to_all(jnp.stack([inputs] * lax.axis_size(TP)), TP, 0, 0)]
    dot_general x0 -> x1, local copies, waits for them, and re-layouts: none -> 6.38 us  [per_device(): jnp.dot(jnp.concatenate(lax.all_to_all(jnp.stack([inputs] * lax.axis_size...]
where the time goes in v1:
time: 402 us; the launch traced here: 401 us
  waiting for transfers between devices  270 us (67%)
  starting transfers between devices  48.4 us (12%)
  local copies, waits for them, and re-layouts  32.1 us (8%)
  matrix products  22.8 us (6%)
  between operations  14.5 us (4%)
  other arithmetic  12.6 us (3%)
    all_to_all x1, waiting for transfers between devices, per_device(): lax.all_to_all(jnp.stack([inputs] * lax.axis_size(TP)), TP, 0, 0)  83.2 us
    all_to_all x6, waiting for transfers between devices, exchange_in_order(): lax.all_to_all(tiles, axes[k], split_axis=k, concat_axis=k, tiled=True)  80.5 us
    all_gather x1, waiting for transfers between devices, per_device(): lax.all_gather(own_attended, TP, axis=1, tiled=True)  56.5 us
    all_gather x1, waiting for transfers between devices, per_device(): queries = lax.all_gather(own_queries, TP, axis=1, tiled=True)  32.1 us
    all_to_all x6, starting transfers between devices, exchange_in_order(): lax.all_to_all(tiles, axes[k], split_axis=k, concat_axis=k, tiled=True)  25.7 us
    all_to_all x1, waiting for transfers between devices, summed_on_arrival(): lax.all_to_all(tiles, axis, split_axis=0, concat_axis=0, tiled=True)  17.5 us
    reshape x2, local copies, waits for them, and re-layouts, per_device(): jnp.concatenate(lax.all_to_all(jnp.stack([inputs] * lax.axis_size(TP)), T...  13.9 us
    all_to_all x1, starting transfers between devices, per_device(): lax.all_to_all(jnp.stack([inputs] * lax.axis_size(TP)), TP, 0, 0)  11.4 us
  transfers between devices with their start and end apart: 11, of which 10 were waited for; matrix products, arithmetic and copies ran while one was open for 8% of the time, Pallas kernels for 0%

profile of v1, /device:TPU:2, one launch (start us, length us, event | category | flops | bytes accessed | tf_op | source)
XLA Modules:
  0.0 400.9 jit_solution(9462508639157181698)
XLA Ops:
  6.5 3.4 stack.10
  10.0 11.4 %all-to-all-start = ((bf16[16,256,512]{2,1,0:T(8,128)(2,1)}), bf16[16,256,512]{2,1,0:T(8,128)(2,1)}, u32[]{:S(2)}, u32[]{:S(2)}) async-start(bf16[16,256,512]{2,1,0:T(8,128)(2,1)} %stack.10), calls=%async_computation | async-start | bytes 8388608 | tf_op jit(solution)/shard_map/all_to_all | solution.py:160
  23.5 6.4 %copy.57 = bf16[256,8192]{1,0:T(8,128)(2,1)} copy(bf16[256,8192]{0,1:T(8,128)(2,1)} %bitcast.110) | data formatting | bytes 8388608 | tf_op jit(solution)/shard_map/dot_general | solution.py:159
  29.8 0.6 dynamic_slice.10
  31.1 0.6 fusion.68
  32.0 83.2 %all-to-all-done = bf16[16,256,512]{2,1,0:T(8,128)(2,1)} async-done(((bf16[16,256,512]{2,1,0:T(8,128)(2,1)}), bf16[16,256,512]{2,1,0:T(8,128)(2,1)}, u32[]{:S(2)}, u32[]{:S(2)}) %all-to-all-start) | async-done | bytes 4194336 | tf_op jit(solution)/shard_map/all_to_all | solution.py:160
  115.2 6.5 %copy.38 = bf16[256,16,512]{2,1,0:T(8,128)(2,1)} copy(bf16[256,16,512]{2,0,1:T(8,128)(2,1)} %bitcast.4) | data formatting | bytes 8388608 | tf_op jit(solution)/shard_map/reshape | solution.py:160
  121.7 7.5 %reshape.502 = bf16[256,8192,1]{1,0,2:T(8,128)(2,1)} reshape(bf16[256,16,512]{2,1,0:T(8,128)(2,1)} %copy.38) | data formatting | bytes 8388608 | tf_op jit(solution)/shard_map/reshape | solution.py:160
  129.2 4.8 %fusion.71 = f32[256,2,128]{0,2,1:T(8,128)S(1)} fusion(bf16[256,8192,1]{1,0,2:T(8,128)(2,1)} %reshape.502, bf16[2,128,8192]{2,1,0:T(8,128)(2,1)} %bitcast.111), kind=kOutput, calls=%fused_computation.152 | convolution fusion | flops 1073741824 | bytes 8650752 | tf_op jit(solution)/shard_map/dot_general | solution.py:159
  134.0 0.7 pad_maximum_fusion.2
  134.7 1.2 convolution_convert_fusion
  135.9 9.9 %all-to-all-start.1 = ((bf16[16,16,1024]{2,1,0:T(8,128)(2,1)}), bf16[16,16,1024]{2,1,0:T(8,128)(2,1)S(1)}, u32[]{:S(2)}, u32[]{:S(2)}) async-start(bf16[16,16,1024]{2,1,0:T(8,128)(2,1)} %bitcast.10), calls=%async_computation.1 | async-start | bytes 1048576 | tf_op jit(solution)/shard_map/all_to_all | solution.py:23
  146.5 0.6 fusion.53
  147.7 17.5 %all-to-all-done.1 = bf16[16,16,1024]{2,1,0:T(8,128)(2,1)S(1)} async-done(((bf16[16,16,1024]{2,1,0:T(8,128)(2,1)}), bf16[16,16,1024]{2,1,0:T(8,128)(2,1)S(1)}, u32[]{:S(2)}, u32[]{:S(2)}) %all-to-all-start.1) | async-done | bytes 524320 | tf_op jit(solution)/shard_map/all_to_all | solution.py:23
  165.5 1.3 collective-permute-start
  167.0 0.6 collective-permute-done
  167.6 0.9 pad_maximum_fusion
  168.5 32.1 %all-gather.3.cloned.1.call-done = bf16[256,4096]{0,1:T(8,128)(2,1)} async-done(((bf16[256,256]{0,1:T(8,128)(2,1)}), bf16[256,4096]{0,1:T(8,128)(2,1)}) %all-gather.3.cloned.1.call-update) | async-done | bytes 2097168 | tf_op jit(solution)/shard_map/all_gather | solution.py:169
  200.5 1.7 fusion.69
  203.2 0.5 fusion
  203.7 3.3 fusion.4
  207.0 0.6 reshape_broadcast_in_dim.6
  207.6 4.7 %all-to-all-start.4 = ((f32[4,4,1,256,2]{3,4,1,2,0:T(2,128)}), f32[4,4,1,256,2]{3,4,1,2,0:T(2,128)S(1)}, u32[]{:S(2)}, u32[]{:S(2)}) async-start(f32[4,4,1,256,2]{3,4,1,2,0:T(2,128)} %bitcast.33), calls=%async_computation.4 | async-start | bytes 65536 | tf_op jit(solution)/shard_map/all_to_all | solution.py:43
  212.3 4.3 %fusion.6 = (f32[256,8]{0,1:T(8,128)S(1)}, f32[256,8]{0,1:T(8,128)S(1)}, f32[256,8]{0,1:T(8,128)S(1)}) fusion(f32[256,8,288]{0,2,1:T(8,128)} %get-tuple-element.32, f32[256,8]{0,1:T(8,128)S(1)} %get-tuple-element.6, pred[256,288]{0,1:T(8,128)(4,1)S(1)} %add_select_fusion, f32[256,8]{0,1:T(8,128)S(1)} %get-tuple-element.7, f32[256,8,288]{0,2,1:T(8,128)} %copy-done.2, ...), kind=kLoop, calls=%fused_computation.17 | loop fusion | flops 8841216 | bytes 7200768 | tf_op jit(solution)/shard_map/reduce_sum | solution.py:100
  216.6 0.8 fusion.12
  217.4 0.9 copy-done.6
  218.3 1.6 fusion.13
  219.9 1.6 fusion.14
  221.5 0.6 reshape_broadcast_in_dim.7
  222.2 7.2 %all-to-all-start.6 = ((f32[4,4,1,256,2]{3,4,1,2,0:T(2,128)}), f32[4,4,1,256,2]{3,4,1,2,0:T(2,128)S(1)}, u32[]{:S(2)}, u32[]{:S(2)}) async-start(f32[4,4,1,256,2]{3,4,1,2,0:T(2,128)} %bitcast.36), calls=%async_computation.6 | async-start | bytes 65536 | tf_op jit(solution)/shard_map/all_to_all | solution.py:43
  229.4 1.6 fusion.15
  231.0 0.6 copy.46
  231.6 5.7 %all-to-all-done.6 = f32[4,4,1,256,2]{3,4,1,2,0:T(2,128)S(1)} async-done(((f32[4,4,1,256,2]{3,4,1,2,0:T(2,128)}), f32[4,4,1,256,2]{3,4,1,2,0:T(2,128)S(1)}, u32[]{:S(2)}, u32[]{:S(2)}) %all-to-all-start.6) | async-done | bytes 32800 | tf_op jit(solution)/shard_map/all_to_all | solution.py:43
  237.2 3.4 all-to-all-start.5
  240.6 2.9 maximum_convert_fusion
  243.6 2.5 all-to-all-done.5
  246.1 3.6 all-to-all-start.2
  249.7 0.6 copy.48
  250.3 45.5 %all-to-all-done.2 = bf16[4,4,1,256,256]{3,4,1,2,0:T(8,128)(2,1)S(1)} async-done(((bf16[4,4,1,256,256]{3,4,1,2,0:T(8,128)(2,1)}), bf16[4,4,1,256,256]{3,4,1,2,0:T(8,128)(2,1)S(1)}, u32[]{:S(2)}, u32[]{:S(2)}) %all-to-all-start.2) | async-done | bytes 2097184 | tf_op jit(solution)/shard_map/all_to_all | solution.py:43
  295.8 3.3 all-to-all-start.7
  299.1 1.5 copy.44
  300.5 3.9 all-to-all-done.7
  304.5 3.6 all-to-all-start.3
  308.3 22.9 %all-to-all-done.3 = bf16[4,4,1,256,256]{3,4,0,2,1:T(8,128)(2,1)S(1)} async-done(((bf16[4,4,1,256,256]{3,4,0,2,1:T(8,128)(2,1)}), bf16[4,4,1,256,256]{3,4,0,2,1:T(8,128)(2,1)S(1)}, u32[]{:S(2)}, u32[]{:S(2)}) %all-to-all-start.3) | async-done | bytes 2097184 | tf_op jit(solution)/shard_map/all_to_all | solution.py:43
  331.5 0.5 multiply_reduce_fusion
  332.0 0.7 fusion.41
  332.8 56.5 %all-gather.5.cloned.1.call-done = bf16[256,4096]{0,1:T(8,128)(2,1)} async-done(((bf16[256,256]{0,1:T(8,128)(2,1)}), bf16[256,4096]{0,1:T(8,128)(2,1)}) %all-gather.5.cloned.1.call-update) | async-done | bytes 2097168 | tf_op jit(solution)/shard_map/all_gather | solution.py:209
  389.3 4.8 %fusion.40 = bf16[1,1,256,512]{3,2,1,0:T(8,128)(2,1)} fusion(bf16[256,4096]{0,1:T(8,128)(2,1)} %all-gather.5.cloned.1.call-done, bf16[4096,512]{1,0:T(8,128)(2,1)} %param.12), kind=kOutput, calls=%fused_computation.53 | convolution fusion | flops 1073872896 | bytes 6553600 | tf_op jit(solution)/shard_map/dot_general | solution.py:208
  (90 shorter events, 5.5 us)
Async XLA Ops:
  6.5 128.1 %copy-start = (bf16[512,1024]{1,0:T(8,128)(2,1)S(1)}, bf16[512,1024]{1,0:T(8,128)(2,1)}, u32[]{:S(2)}) copy-start(bf16[512,1024]{1,0:T(8,128)(2,1)} %param.11) | copy-start | bytes 3145732
  10.0 11.5 %copy-start.12 = (s32[1,4,64]{2,1,0:T(4,128)S(1)}, s32[1,4,64]{2,1,0:T(4,128)}, u32[]{:S(2)}) copy-start(s32[1,4,64]{2,1,0:T(4,128)} %param.17) | copy-start | bytes 3076
  10.0 13.3 %copy-start.13 = (s32[1,4]{1,0:T(1,128)S(1)}, s32[1,4]{1,0:T(1,128)}, u32[]{:S(2)}) copy-start(s32[1,4]{1,0:T(1,128)} %param.16) | copy-start | bytes 52
  10.0 105.2 %all-to-all-start = ((bf16[16,256,512]{2,1,0:T(8,128)(2,1)}), bf16[16,256,512]{2,1,0:T(8,128)(2,1)}, u32[]{:S(2)}, u32[]{:S(2)}) async-start(bf16[16,256,512]{2,1,0:T(8,128)(2,1)} %stack.10), calls=%async_computation | async-start | bytes 8388608 | tf_op jit(solution)/shard_map/all_to_all | solution.py:160
  21.3 179.2 %all-gather.3.cloned.1.call-start = ((), (), s32[]{:S(2)}) async-start(), calls=%async_computation.8 | async-start | bytes 2228224 | tf_op jit(solution)/shard_map/all_gather | solution.py:169
  23.5 6.4 %copy-start.14 = (s32[8]{0:T(128)S(1)}, s32[8]{0:T(128)}, u32[]{:S(2)}) copy-start(s32[8]{0:T(128)} %param.15) | copy-start | bytes 100
  129.2 5.5 %copy-start.7 = (bf16[1,1,256,512]{3,2,1,0:T(8,128)(2,1)S(1)}, bf16[1,1,256,512]{3,2,1,0:T(8,128)(2,1)}, u32[]{:S(2)}) copy-start(bf16[1,1,256,512]{3,2,1,0:T(8,128)(2,1)} %param.9) | copy-start | bytes 786436
  135.9 31.7 %copy-start.10 = (bf16[1,1,256,512]{3,2,1,0:T(8,128)(2,1)S(1)}, bf16[1,1,256,512]{3,2,1,0:T(8,128)(2,1)}, u32[]{:S(2)}) copy-start(bf16[1,1,256,512]{3,2,1,0:T(8,128)(2,1)} %param.13) | copy-start | bytes 786436
  135.9 31.7 %copy-start.11 = (bf16[1,1,256,512]{3,2,1,0:T(8,128)(2,1)S(1)}, bf16[1,1,256,512]{3,2,1,0:T(8,128)(2,1)}, u32[]{:S(2)}) copy-start(bf16[1,1,256,512]{3,2,1,0:T(8,128)(2,1)} %param.14) | copy-start | bytes 786436
  135.9 29.2 %all-to-all-start.1 = ((bf16[16,16,1024]{2,1,0:T(8,128)(2,1)}), bf16[16,16,1024]{2,1,0:T(8,128)(2,1)S(1)}, u32[]{:S(2)}, u32[]{:S(2)}) async-start(bf16[16,16,1024]{2,1,0:T(8,128)(2,1)} %bitcast.10), calls=%async_computation.1 | async-start | bytes 1048576 | tf_op jit(solution)/shard_map/all_to_all | solution.py:23
  165.5 2.1 collective-permute-start
  200.5 1.7 copy-start.8
  203.2 3.8 copy-start.2
  203.7 3.3 copy-start.4
  207.6 14.5 %all-to-all-start.4 = ((f32[4,4,1,256,2]{3,4,1,2,0:T(2,128)}), f32[4,4,1,256,2]{3,4,1,2,0:T(2,128)S(1)}, u32[]{:S(2)}, u32[]{:S(2)}) async-start(f32[4,4,1,256,2]{3,4,1,2,0:T(2,128)} %bitcast.33), calls=%async_computation.4 | async-start | bytes 65536 | tf_op jit(solution)/shard_map/all_to_all | solution.py:43
  212.3 4.3 %copy-start.5 = (f32[256,8,288]{0,2,1:T(8,128)S(1)}, f32[256,8,288]{0,2,1:T(8,128)}, u32[]{:S(2)}) copy-start(f32[256,8,288]{0,2,1:T(8,128)} %copy-done.4) | copy-start | bytes 7077892
  212.3 4.3 %copy-start.9 = (bf16[288,512]{1,0:T(8,128)(2,1)S(1)}, bf16[288,512]{1,0:T(8,128)(2,1)}, u32[]{:S(2)}) copy-start(bf16[288,512]{1,0:T(8,128)(2,1)} %get-tuple-element.38) | copy-start | bytes 884740
  216.6 1.7 copy-start.6
  218.3 1.7 copy-start.3
  222.2 15.1 %all-to-all-start.6 = ((f32[4,4,1,256,2]{3,4,1,2,0:T(2,128)}), f32[4,4,1,256,2]{3,4,1,2,0:T(2,128)S(1)}, u32[]{:S(2)}, u32[]{:S(2)}) async-start(f32[4,4,1,256,2]{3,4,1,2,0:T(2,128)} %bitcast.36), calls=%async_computation.6 | async-start | bytes 65536 | tf_op jit(solution)/shard_map/all_to_all | solution.py:43
  237.2 8.8 %all-to-all-start.5 = ((f32[4,4,1,256,2]{3,4,0,2,1:T(2,128)}), f32[4,4,1,256,2]{3,4,0,2,1:T(2,128)S(1)}, u32[]{:S(2)}, u32[]{:S(2)}) async-start(f32[4,4,1,256,2]{3,4,0,2,1:T(2,128)} %copy.46), calls=%async_computation.5 | async-start | bytes 65536 | tf_op jit(solution)/shard_map/all_to_all | solution.py:43
  246.1 49.7 %all-to-all-start.2 = ((bf16[4,4,1,256,256]{3,4,1,2,0:T(8,128)(2,1)}), bf16[4,4,1,256,256]{3,4,1,2,0:T(8,128)(2,1)S(1)}, u32[]{:S(2)}, u32[]{:S(2)}) async-start(bf16[4,4,1,256,256]{3,4,1,2,0:T(8,128)(2,1)} %bitcast.109), calls=%async_computation.2 | async-start | bytes 4194304 | tf_op jit(solution)/shard_map/all_to_all | solution.py:43
  295.8 8.7 %all-to-all-start.7 = ((f32[4,4,1,256,2]{3,4,0,2,1:T(2,128)}), f32[4,4,1,256,2]{3,4,0,2,1:T(2,128)S(1)}, u32[]{:S(2)}, u32[]{:S(2)}) async-start(f32[4,4,1,256,2]{3,4,0,2,1:T(2,128)} %copy.48), calls=%async_computation.7 | async-start | bytes 65536 | tf_op jit(solution)/shard_map/all_to_all | solution.py:43
  304.5 26.7 %all-to-all-start.3 = ((bf16[4,4,1,256,256]{3,4,0,2,1:T(8,128)(2,1)}), bf16[4,4,1,256,256]{3,4,0,2,1:T(8,128)(2,1)S(1)}, u32[]{:S(2)}, u32[]{:S(2)}) async-start(bf16[4,4,1,256,256]{3,4,0,2,1:T(8,128)(2,1)} %copy.44), calls=%async_computation.3 | async-start | bytes 4194304 | tf_op jit(solution)/shard_map/all_to_all | solution.py:43
  308.1 81.2 %all-gather.5.cloned.1.call-start = ((), (), s32[]{:S(2)}) async-start(), calls=%async_computation.9 | async-start | bytes 2228224 | tf_op jit(solution)/shard_map/all_gather | solution.py:209
  332.7 61.3 %copy-start.1 = (bf16[512,1024]{1,0:T(8,128)(2,1)S(1)}, bf16[512,1024]{1,0:T(8,128)(2,1)}, u32[]{:S(2)}) copy-start(bf16[512,1024]{1,0:T(8,128)(2,1)} %param.11) | copy-start | bytes 3145732
Sparse Core Ops, SparseCore 0:
  134.8 65.7 all-gather.2
  332.9 56.3 all-gather.4
